TPU v7x, 256 devices: a whole 4x4x8 slice. The times are simulated.
256 devices in a mesh: ctx: 32 (over x, y, core), tp: 8 (over z).
Axes of the slice: x: 4, y: 4, z: 8, core: 2. Of those that a mesh axis runs over, the one named last changes fastest.
Arguments:
- patches: bfloat16 [16384, 1280], P('ctx'), may hold values from -21 to 21
- window_ids: int32 [16384], P('ctx'), may hold values from -1 to 4095, as said below
- positions: int32 [4096], P('ctx'), may hold values from 0 to 32768, as said below
- text_embed: bfloat16 [32768, 8192], P('ctx', 'tp'), may hold values from -6 to 6
- cotangent: bfloat16 [32768, 8192], P('ctx', 'tp'), may hold values from -0.119628906 to 0.119628906
- qkv_weight: bfloat16 [3, 1280, 1280], P(None, None, 'tp'), may hold values from -0.15625 to 0.15625
- out_weight: bfloat16 [1280, 1280], P('tp'), may hold values from -0.15625 to 0.15625
- merger_weight: bfloat16 [5120, 8192], P('ctx', 'tp'), may hold values from -0.078125 to 0.078125
- norm_gain: bfloat16 [8192], P('tp'), may hold values from 0.099609375 to 1.8984375
Outputs:
- normed: bfloat16 [32768, 8192], P('ctx', 'tp')
- merger_grad: float32 [5120, 8192], P('ctx', 'tp')
Inputs may be any that keep to these rules, and one draw needn't show every extreme that they name: `window_ids`: windows are runs of consecutive patch slots of one index of ctx, each of 4 to 64 slots and a multiple of 4; every window id belongs to one index of ctx; the padding slots of an index of ctx come after its live slots and carry -1. Merged slot j of an index of ctx covers its patch slots 4j to 4j+3 and is live exactly when those are; live slots carry distinct positions, dead ones carry 32768. The live slots of one index of ctx name at most 4 positions among the 1024 positions of any one index of ctx.
All inputs are finite; a program needn't handle non-finite values.
Results may differ from a plain program's by a relative error of at most 0.014.
Values may be sent and summed in bfloat16 or wider, within the bound.
A program may use at most 128 MiB of HBM per device.

v0:
```python
import jax
import jax.numpy as jnp
from jax import lax
from jax.sharding import PartitionSpec as P

D = 8192
HEAD_DIM = 80


def sent_to_all(shard, axis):
    copies = jnp.broadcast_to(shard, (lax.axis_size(axis), *shard.shape))
    return lax.all_to_all(copies, axis, split_axis=0, concat_axis=0, tiled=True)


def taken_together(shard, axis):
    return sent_to_all(shard, axis).sum(axis=0)


def in_one(arrays, axis):
    ends = [0]
    for a in arrays:
        ends.append(ends[-1] + a.size)
    so_far = taken_together(jnp.concatenate([a.ravel() for a in arrays]), axis)
    return tuple((so_far[b:e].reshape(a.shape) for a, b, e in zip(arrays, ends, ends[1:])))


def window_attention(patches, window_ids, qkv_weight):
    slot_rows = patches.shape[0]
    projected = [
        jnp.dot(patches, qkv_weight[i], preferred_element_type=jnp.float32).astype(jnp.bfloat16)
        for i in range(3)
    ]
    local_heads = qkv_weight.shape[2] // HEAD_DIM
    queries = projected[0].reshape(slot_rows, local_heads, HEAD_DIM)
    keys_all = projected[1].reshape(slot_rows, local_heads, HEAD_DIM)
    values = projected[2].reshape(slot_rows, local_heads, HEAD_DIM)
    width = min(512, slot_rows)
    factor = 1.0 / HEAD_DIM**0.5

    def one_block(block_index):
        scores = (
            jnp.einsum("qhd,khd->hqk", queries, keys_all, preferred_element_type=jnp.float32)
            * factor
        )
        allowed = (window_ids[:, None] == window_ids[None, :]) & (window_ids[None, :] >= 0)
        scores = jnp.where(allowed[None], scores, jnp.float32(-1e30))
        highest = jnp.max(scores, axis=2, keepdims=True)
        weights = jnp.exp(scores - highest)
        probs = (weights / jnp.sum(weights, axis=2, keepdims=True)).astype(jnp.bfloat16)
        attended = jnp.einsum("hqk,khd->qhd", probs, values, preferred_element_type=jnp.float32)
        return attended.astype(jnp.bfloat16).reshape(width, local_heads * HEAD_DIM)

    blocks = lax.map(one_block, jnp.arange(slot_rows // width, dtype=jnp.int32))
    return blocks.reshape(slot_rows, local_heads * HEAD_DIM)


def contract_rows(left, right):
    return lax.dot_general(
        left, right, (((0,), (0,)), ((), ())), preferred_element_type=jnp.float32
    )


def shards(
    patches,
    window_ids,
    positions,
    text_embed,
    cotangent,
    qkv_weight,
    out_weight,
    merger_weight,
    norm_gain,
):
    ctx_size = lax.axis_size("ctx")
    slots = positions.shape[0]
    tok_rows = text_embed.shape[0]
    bucket_size = slots // ctx_size
    attended = window_attention(patches, window_ids, qkv_weight)
    partial_out = jnp.dot(attended, out_weight, preferred_element_type=jnp.float32)
    summed = lax.psum(partial_out.astype(jnp.bfloat16), "tp").astype(jnp.float32)
    hidden = (patches.astype(jnp.float32) + summed).astype(jnp.bfloat16)
    merged_in = hidden.reshape(slots, 4 * hidden.shape[1])
    columns = lax.all_to_all(merged_in, "ctx", split_axis=1, concat_axis=0, tiled=True)
    chosen = merged_in
    merged = jnp.dot(
        chosen,
        lax.all_gather(merger_weight, "ctx", axis=0, tiled=True),
        preferred_element_type=jnp.float32,
    ).astype(jnp.bfloat16)
    target = positions // tok_rows
    hits = (target[:, None] == jnp.arange(ctx_size, dtype=jnp.int32)[None, :]).astype(jnp.int32)
    ranks = jnp.sum(jnp.cumsum(hits, axis=0) * hits, axis=1) - 1
    bucket = jnp.where(target < ctx_size, target * bucket_size + ranks, -1)
    select = jnp.arange(slots, dtype=jnp.int32)[:, None] == bucket[None, :]
    select_mat = select.astype(jnp.bfloat16)
    outgoing = jnp.dot(select_mat, merged, preferred_element_type=jnp.float32).astype(jnp.bfloat16)
    local_row = positions % tok_rows
    occupied = jnp.any(select, axis=1)
    out_rows = jnp.where(occupied, jnp.sum(jnp.where(select, local_row[None, :], 0), axis=1), -1)
    incoming, in_rows = (
        lax.all_to_all(outgoing, "ctx", split_axis=0, concat_axis=0, tiled=True),
        lax.all_to_all(out_rows, "ctx", split_axis=0, concat_axis=0, tiled=True),
    )
    placed = jnp.arange(tok_rows, dtype=jnp.int32)[:, None] == in_rows[None, :]
    placed_mat = placed.astype(jnp.bfloat16)
    vision = jnp.dot(placed_mat, incoming, preferred_element_type=jnp.float32)
    is_vision = jnp.any(placed, axis=1)
    embedded = jnp.where(is_vision[:, None], vision, text_embed.astype(jnp.float32))
    gain_vec = norm_gain.astype(jnp.float32)[None, :]
    gained = gain_vec * cotangent.astype(jnp.float32)
    squares, inner = in_one(
        (jnp.sum(embedded * embedded, axis=1), jnp.sum(embedded * gained, axis=1)), "tp"
    )
    scale = lax.rsqrt(squares / D + 1e-06)[:, None]
    normed = (embedded * scale * gain_vec).astype(jnp.bfloat16)
    d_embed = (scale * gained - embedded * scale**3 * inner[:, None] / D).astype(jnp.bfloat16)
    back_rows = contract_rows(placed_mat, d_embed).astype(jnp.bfloat16)
    returned = lax.all_to_all(back_rows, "ctx", split_axis=0, concat_axis=0, tiled=True)
    d_merged = contract_rows(select_mat, returned).astype(jnp.bfloat16)
    chosen = columns
    merger_grad = contract_rows(chosen, lax.all_gather(d_merged, "ctx", axis=0, tiled=True))
    return (normed, merger_grad)


def solution(mesh):
    in_specs = (
        P("ctx", None),
        P("ctx"),
        P("ctx"),
        P("ctx", "tp"),
        P("ctx", "tp"),
        P(None, None, "tp"),
        P("tp", None),
        P("ctx", "tp"),
        P("tp"),
    )
    out_specs = (P("ctx", "tp"), P("ctx", "tp"))
    return jax.shard_map(shards, mesh=mesh, in_specs=in_specs, out_specs=out_specs, check_vma=False)
```

profile of v0, /device:TPU:1, one launch (start us, length us, event | category | flops | bytes accessed | tf_op | source)
XLA Modules:
  0.0 239.2 jit_solution(6177392035362610401)
XLA Ops:
  8.1 2.1 convolution_convert_fusion.7
  10.2 2.0 convolution_convert_fusion.5
  12.2 1.6 convolution_convert_fusion.6
  15.0 1.2 convolution_convert_fusion.4
  16.3 1.6 convolution_convert_fusion
  19.9 8.6 %all-to-all-start = ((s32[32,4,1]{1,2,0:T(1,128)}), s32[32,4,1]{1,2,0:T(1,128)S(1)}, u32[]{:S(2)}, u32[]{:S(2)}) async-start(s32[32,4,1]{1,2,0:T(1,128)} %bitcast), calls=%async_computation | async-start | bytes 32768 | tf_op jit(solution)/shard_map/all_to_all | solution.py:102
  28.5 66.8 %all-reduce.2.cloned.1.call-done = bf16[512,1280]{1,0:T(8,128)(2,1)} async-done(((bf16[512,1280]{1,0:T(8,128)(2,1)}), bf16[512,1280]{1,0:T(8,128)(2,1)}) %all-reduce.2.cloned.1.call-update) | async-done | bytes 1310736 | tf_op jit(solution)/shard_map/psum | solution.py:80
  95.3 1.6 add_convert_fusion
  97.8 5.7 %convolution_convert_fusion.2 = bf16[128,1024]{1,0:T(8,128)(2,1)S(1)} fusion(bf16[128,5120]{1,0:T(8,128)(2,1)S(1)} %reshape.118, bf16[5120,1024]{1,0:T(8,128)(2,1)} %all-gather.3.cloned.1.call-done, s32[128]{0:T(128)S(1)} %compare_select_fusion), kind=kOutput, calls=%fused_computation.19 | convolution fusion | flops 1376010240 | bytes 12059136 | tf_op jit(solution)/shard_map/dot_general | solution.py:96
  104.3 11.4 %all-to-all-start.1 = ((bf16[32,4,1024]{2,1,0:T(4,128)(2,1)}), bf16[32,4,1024]{2,1,0:T(4,128)(2,1)S(1)}, u32[]{:S(2)}, u32[]{:S(2)}) async-start(bf16[32,4,1024]{2,1,0:T(4,128)(2,1)} %all_to_all.39), calls=%async_computation.1 | async-start | bytes 524288 | tf_op jit(solution)/shard_map/all_to_all | solution.py:101
  115.8 3.9 %copy.37 = bf16[1024,1024]{0,1:T(8,128)(2,1)} copy(bf16[1024,1024]{1,0:T(8,128)(2,1)} %param.13) | data formatting | bytes 4194304 | tf_op args[4]
  119.7 4.0 %copy.36 = bf16[1024,1024]{0,1:T(8,128)(2,1)} copy(bf16[1024,1024]{1,0:T(8,128)(2,1)} %param.12) | data formatting | bytes 4194304 | tf_op args[3]
  125.2 5.6 %multiply_reduce_fusion.1 = (f32[1024]{0:T(1024)S(1)}, f32[1024]{0:T(1024)S(1)}, f32[1024,1024]{0,1:T(8,128)}) fusion(bf16[1024,1024]{0,1:T(8,128)(2,1)} %copy.37, f32[1024]{0:T(1024)S(1)} %convert_element_type.78, bf16[1024,1024]{0,1:T(8,128)(2,1)} %copy.36, bf16[128,1024]{1,0:T(8,128)(2,1)S(1)} %all_to_all.41, s32[128]{0:T(128)S(1)} %eq.74, ...), kind=kOutput, calls=%fused_computation.5 | convolution fusion | flops 276953088 | bytes 8664576 | tf_op jit(solution)/shard_map/dot_general | solution.py:106
  130.9 11.2 %all_to_all.55 = f32[8,1,2048]{2,1,0:T(1,128)S(1)} all-to-all(f32[8,1,2048]{2,1,0:T(1,128)S(1)} %broadcast_in_dim.73), channel_id=1, replica_groups=mesh['ctx'=32,'tp'=8] {'tp'}, dimensions={0} | all-to-all | bytes 131072 | tf_op jit(solution)/shard_map/all_to_all | solution.py:12
  142.2 4.3 %fusion.6 = bf16[128,1024]{1,0:T(8,128)(2,1)S(1)} fusion(f32[1024,1024]{0,1:T(8,128)} %get-tuple-element.37, bf16[1024,1024]{0,1:T(8,128)(2,1)} %copy.37, f32[1024]{0:T(1024)S(1)} %get-tuple-element.34, f32[1024]{0:T(1024)S(1)} %get-tuple-element.32, f32[1024]{0:T(1024)S(1)} %get-tuple-element.33, f32[1024]{0:T(1024)S(1)} %convert_element_type.78, ...), kind=kOutput, calls=%fused_computation.17 | convolution fusion | flops 277217280 | bytes 6570496 | tf_op jit(solution)/shard_map/dot_general | solution.py:58
  146.5 17.6 %all_to_all.56 = bf16[32,4,1024]{2,1,0:T(4,128)(2,1)S(1)} all-to-all(bf16[32,4,1024]{2,1,0:T(4,128)(2,1)S(1)} %all_to_all.47), channel_id=1, replica_groups=mesh['ctx'=32,'tp'=8] {'ctx'}, dimensions={0} | all-to-all | bytes 524288 | tf_op jit(solution)/shard_map/all_to_all | solution.py:118
  165.2 3.6 %all_to_all.43 = bf16[128,32,160]{2,1,0:T(8,128)(2,1)} reshape(bf16[512,1280]{1,0:T(8,128)(2,1)S(1)} %add_convert_fusion) | data formatting | bytes 2621440 | tf_op jit(solution)/shard_map/all_to_all | solution.py:83
  168.8 4.4 %copy.39 = bf16[128,32,160]{0,2,1:T(8,128)(2,1)} copy(bf16[128,32,160]{2,1,0:T(8,128)(2,1)} %all_to_all.43) | data formatting | bytes 2621440 | tf_op jit(solution)/shard_map/all_to_all | solution.py:83
  173.2 4.5 %all-to-all-start.3 = ((bf16[128,32,160]{0,2,1:T(8,128)(2,1)}), bf16[128,32,160]{0,2,1:T(8,128)(2,1)}, u32[]{:S(2)}, u32[]{:S(2)}) async-start(bf16[128,32,160]{0,2,1:T(8,128)(2,1)} %copy.39), calls=%async_computation.3 | async-start | bytes 2621440 | tf_op jit(solution)/shard_map/all_to_all | solution.py:83
  177.7 2.6 %multiply_convert_fusion = bf16[1024,1024]{0,1:T(8,128)(2,1)S(1)} fusion(f32[1024,1024]{0,1:T(8,128)} %get-tuple-element.37, f32[1024]{0:T(1024)S(1)} %get-tuple-element.33, f32[1024]{0:T(1024)S(1)} %convert_element_type.78), kind=kLoop, calls=%fused_computation.2 | loop fusion | flops 3145728 | bytes 6299648 | tf_op jit(solution)/shard_map/convert_element_type | solution.py:115
  180.3 2.6 %copy.41 = bf16[1024,1024]{1,0:T(8,128)(2,1)} copy(bf16[1024,1024]{0,1:T(8,128)(2,1)S(1)} %multiply_convert_fusion) | data formatting | bytes 4194304
  182.9 15.3 %all-to-all-done.3 = bf16[128,32,160]{0,2,1:T(8,128)(2,1)} async-done(((bf16[128,32,160]{0,2,1:T(8,128)(2,1)}), bf16[128,32,160]{0,2,1:T(8,128)(2,1)}, u32[]{:S(2)}, u32[]{:S(2)}) %all-to-all-start.3) | async-done | bytes 1310752 | tf_op jit(solution)/shard_map/all_to_all | solution.py:83
  198.2 27.4 %all-gather.5.cloned.1.call-done = bf16[4096,1024]{1,0:T(8,128)(2,1)} async-done(((bf16[128,1024]{1,0:T(8,128)(2,1)}), bf16[4096,1024]{1,0:T(8,128)(2,1)}) %all-gather.5.cloned.1.call-update) | async-done | bytes 8388624 | tf_op jit(solution)/shard_map/all_gather | solution.py:121
  225.6 6.2 %fusion.3 = f32[160,1024]{1,0:T(8,128)} fusion(bf16[4096,1024]{1,0:T(8,128)(2,1)} %all-gather.5.cloned.1.call-done, bf16[128,32,160]{0,2,1:T(8,128)(2,1)} %all-to-all-done.3), kind=kOutput, calls=%fused_computation.14 | convolution fusion | flops 1342177280 | bytes 10354688 | tf_op jit(solution)/shard_map/dot_general | solution.py:58
  (46 shorter events, 7.8 us)
Async XLA Ops:
  8.0 8.3 %copy-start = (bf16[160,1280]{1,0:T(8,128)(2,1)S(1)}, bf16[160,1280]{1,0:T(8,128)(2,1)}, u32[]{:S(2)}) copy-start(bf16[160,1280]{1,0:T(8,128)(2,1)} %param.15) | copy-start | bytes 1228804
  8.0 4.1 %copy-start.1 = (bf16[512,1280]{1,0:T(8,128)(2,1)S(1)}, bf16[512,1280]{1,0:T(8,128)(2,1)}, u32[]{:S(2)}) copy-start(bf16[512,1280]{1,0:T(8,128)(2,1)} %param.9) | copy-start | bytes 3932164
  8.0 87.3 %all-reduce.2.cloned.1.call-start = ((), (), s32[]{:S(2)}) async-start(), calls=%async_computation.5 | async-start | bytes 2621440 | tf_op jit(solution)/shard_map/psum | solution.py:80
  10.2 3.6 %copy-start.2 = (s32[512]{0:T(512)S(1)}, s32[512]{0:T(512)}, u32[]{:S(2)}) copy-start(s32[512]{0:T(512)} %param.10) | copy-start | bytes 6148
  16.2 2.2 copy-start.4
  17.9 79.9 %all-gather.3.cloned.1.call-start = ((), (), s32[]{:S(2)}) async-start(), calls=%async_computation.6 | async-start | bytes 10813440 | tf_op jit(solution)/shard_map/all_gather | solution.py:87
  19.9 84.4 %all-to-all-start = ((s32[32,4,1]{1,2,0:T(1,128)}), s32[32,4,1]{1,2,0:T(1,128)S(1)}, u32[]{:S(2)}, u32[]{:S(2)}) async-start(s32[32,4,1]{1,2,0:T(1,128)} %bitcast), calls=%async_computation | async-start | bytes 32768 | tf_op jit(solution)/shard_map/all_to_all | solution.py:102
  97.8 18.0 %copy-start.3 = (bf16[1024]{0:T(1024)(128)(2,1)S(1)}, bf16[1024]{0:T(1024)(128)(2,1)}, u32[]{:S(2)}) copy-start(bf16[1024]{0:T(1024)(128)(2,1)} %param.17) | copy-start | bytes 6148
  104.3 20.9 %all-to-all-start.1 = ((bf16[32,4,1024]{2,1,0:T(4,128)(2,1)}), bf16[32,4,1024]{2,1,0:T(4,128)(2,1)S(1)}, u32[]{:S(2)}, u32[]{:S(2)}) async-start(bf16[32,4,1024]{2,1,0:T(4,128)(2,1)} %all_to_all.39), calls=%async_computation.1 | async-start | bytes 524288 | tf_op jit(solution)/shard_map/all_to_all | solution.py:101
  115.7 109.9 %all-gather.5.cloned.1.call-start = ((), (), s32[]{:S(2)}) async-start(), calls=%async_computation.7 | async-start | bytes 8650752 | tf_op jit(solution)/shard_map/all_gather | solution.py:121
  173.2 25.0 %all-to-all-start.3 = ((bf16[128,32,160]{0,2,1:T(8,128)(2,1)}), bf16[128,32,160]{0,2,1:T(8,128)(2,1)}, u32[]{:S(2)}, u32[]{:S(2)}) async-start(bf16[128,32,160]{0,2,1:T(8,128)(2,1)} %copy.39), calls=%async_computation.3 | async-start | bytes 2621440 | tf_op jit(solution)/shard_map/all_to_all | solution.py:83
Sparse Core Ops, SparseCore 0:
  18.0 77.2 all-reduce.1
Sparse Core Ops, SparseCore 1:
  20.9 66.7 all-gather.2
  165.3 60.3 all-gather.4
where the time goes:
time: 240 us; the launch traced here: 239 us
  waiting for transfers between devices  110 us (46%)
  matrix products  32.1 us (13%)
  blocking collectives  28.8 us (12%)
  starting transfers between devices  24.6 us (10%)
  local copies, waits for them, and re-layouts  21.8 us (9%)
  between operations  15.8 us (7%)
  other arithmetic  6.13 us (3%)
    psum x1, waiting for transfers between devices, shards(): lax.psum(partial_out.astype(jnp.bfloat16), 'tp').astype(jnp.float32)  66.8 us
    all_gather x1, waiting for transfers between devices, shards(): lax.all_gather(d_merged, 'ctx', axis=0, tiled=True)  27.4 us
    all_to_all x1, blocking collectives, shards(): lax.all_to_all(back_rows, 'ctx', split_axis=0, concat_axis=0, tiled=True)  17.6 us
    all_to_all x1, waiting for transfers between devices, shards(): lax.all_to_all(merged_in, 'ctx', split_axis=1, concat_axis=0, tiled=True)  15.3 us
    all_to_all x1, starting transfers between devices, shards(): lax.all_to_all(outgoing, 'ctx', split_axis=0, concat_axis=0, tiled=True)  11.4 us
    dot_general x3, matrix products, contract_rows(): lax.dot_general(left, right, (((0,), (0,)), ((), ())), preferred_element_...  11.4 us
    all_to_all x1, blocking collectives, sent_to_all(): return lax.all_to_all(copies, axis, split_axis=0, concat_axis=0, tiled=True)  11.2 us
    unnamed x13, local copies, waits for them, and re-layouts  10.5 us
  transfers between devices with their start and end apart: 6, of which 3 were waited for; matrix products, arithmetic and copies ran while one was open for 12% of the time, Pallas kernels for 0%

commit v1 on v0

--- a/solution.py
+++ b/solution.py
@@ -5,6 +5,10 @@
 
 D = 8192
 HEAD_DIM = 80
+
+
+def desk_part(work_x):
+    return jnp.sum(lax.all_gather(work_x, "tp"), axis=0)
 
 
 def sent_to_all(shard, axis):
@@ -77,7 +81,7 @@
     bucket_size = slots // ctx_size
     attended = window_attention(patches, window_ids, qkv_weight)
     partial_out = jnp.dot(attended, out_weight, preferred_element_type=jnp.float32)
-    summed = lax.psum(partial_out.astype(jnp.bfloat16), "tp").astype(jnp.float32)
+    summed = desk_part(partial_out.astype(jnp.bfloat16)).astype(jnp.float32)
     hidden = (patches.astype(jnp.float32) + summed).astype(jnp.bfloat16)
     merged_in = hidden.reshape(slots, 4 * hidden.shape[1])
     columns = lax.all_to_all(merged_in, "ctx", split_axis=1, concat_axis=0, tiled=True)

time: 240 us -> 337 us (1.40)
  waiting for transfers between devices: 110 us -> 206 us
  other arithmetic: 6.13 us -> 12.4 us
  starting transfers between devices: 24.6 us -> 18.8 us
    all_gather x0 -> x1, waiting for transfers between devices: none -> 107 us  [desk_part(): return jnp.sum(lax.all_gather(work_x, 'tp'), axis=0)]
    psum x1 -> x0, waiting for transfers between devices: 66.8 us -> none  [shards(): lax.psum(partial_out.astype(jnp.bfloat16), 'tp').astype(jnp.float32)]
    all_gather x1, waiting for transfers between devices: 0.03 us -> 55.7 us  [shards(): lax.all_gather(merger_weight, 'ctx', axis=0, tiled=True)]
    reduce_sum x0 -> x1, other arithmetic: none -> 6.23 us  [desk_part(): return jnp.sum(lax.all_gather(work_x, 'tp'), axis=0)]
    all_to_all x1, starting transfers between devices: 11.4 us -> 5.46 us  [shards(): lax.all_to_all(outgoing, 'ctx', split_axis=0, concat_axis=0, tiled=True)]
  transfers between devices with their start and end apart: 6 -> 6, of which waited for: 3 -> 4; matrix products, arithmetic and copies ran while one was open for 12% -> 10% of each run, Pallas kernels for 0% -> 0%
where the time goes in v1:
time: 337 us; the launch traced here: 336 us
  waiting for transfers between devices  206 us (61%)
  matrix products  32.1 us (10%)
  blocking collectives  31.3 us (9%)
  local copies, waits for them, and re-layouts  21.8 us (6%)
  starting transfers between devices  18.8 us (6%)
  between operations  14 us (4%)
  other arithmetic  12.4 us (4%)
    all_gather x1, waiting for transfers between devices, desk_part(): return jnp.sum(lax.all_gather(work_x, 'tp'), axis=0)  107 us
    all_gather x1, waiting for transfers between devices, shards(): lax.all_gather(merger_weight, 'ctx', axis=0, tiled=True)  55.7 us
    all_gather x1, waiting for transfers between devices, shards(): lax.all_gather(d_merged, 'ctx', axis=0, tiled=True)  27.3 us
    all_to_all x1, blocking collectives, shards(): lax.all_to_all(back_rows, 'ctx', split_axis=0, concat_axis=0, tiled=True)  17.6 us
    all_to_all x1, waiting for transfers between devices, shards(): lax.all_to_all(merged_in, 'ctx', split_axis=1, concat_axis=0, tiled=True)  15.4 us
    all_to_all x1, blocking collectives, sent_to_all(): return lax.all_to_all(copies, axis, split_axis=0, concat_axis=0, tiled=True)  13.8 us
    dot_general x3, matrix products, contract_rows(): lax.dot_general(left, right, (((0,), (0,)), ((), ())), preferred_element_...  11.4 us
    unnamed x13, local copies, waits for them, and re-layouts  10.5 us
  transfers between devices with their start and end apart: 6, of which 4 were waited for; matrix products, arithmetic and copies ran while one was open for 10% of the time, Pallas kernels for 0%

profile of v1, /device:TPU:1, one launch (start us, length us, event | category | flops | bytes accessed | tf_op | source)
XLA Modules:
  0.0 336.3 jit_solution(6236507039545012990)
XLA Ops:
  7.2 2.1 convolution_convert_fusion.6
  9.3 2.0 convolution_convert_fusion.5
  15.4 1.6 convolution_convert_fusion
  19.3 8.6 %all-to-all-start = ((s32[32,4,1]{1,2,0:T(1,128)}), s32[32,4,1]{1,2,0:T(1,128)S(1)}, u32[]{:S(2)}, u32[]{:S(2)}) async-start(s32[32,4,1]{1,2,0:T(1,128)} %bitcast), calls=%async_computation | async-start | bytes 32768 | tf_op jit(solution)/shard_map/all_to_all | solution.py:106
  27.8 106.7 %all-gather.9.cloned.1.call-done = bf16[4096,1280]{1,0:T(8,128)(2,1)} async-done(((bf16[512,1280]{1,0:T(8,128)(2,1)}), bf16[4096,1280]{1,0:T(8,128)(2,1)}) %all-gather.9.cloned.1.call-update) | async-done | bytes 10485776 | tf_op jit(solution)/shard_map/all_gather | solution.py:11
  134.6 6.2 %reduce_sum.70 = bf16[512,1280]{1,0:T(8,128)(2,1)S(1)} reduce(bf16[8,512,1280]{2,1,0:T(8,128)(2,1)} %bitcast.41, bf16[]{:T(256)} %constant.69.clone.1), dimensions={0}, to_apply=%region_7.8 | reduce | flops 4587520 | bytes 11796482 | tf_op jit(solution)/shard_map/reduce_sum | solution.py:11
  140.8 1.6 add_convert_fusion
  143.3 55.7 %all-gather.5.cloned.1.call-done = bf16[5120,1024]{1,0:T(8,128)(2,1)} async-done(((bf16[160,1024]{1,0:T(8,128)(2,1)}), bf16[5120,1024]{1,0:T(8,128)(2,1)}) %all-gather.5.cloned.1.call-update) | async-done | bytes 10485776 | tf_op jit(solution)/shard_map/all_gather | solution.py:91
  199.0 5.7 %convolution_convert_fusion.2 = bf16[128,1024]{1,0:T(8,128)(2,1)S(1)} fusion(bf16[128,5120]{1,0:T(8,128)(2,1)S(1)} %reshape.118, bf16[5120,1024]{1,0:T(8,128)(2,1)} %all-gather.5.cloned.1.call-done, s32[128]{0:T(128)S(1)} %compare_select_fusion), kind=kOutput, calls=%fused_computation.19 | convolution fusion | flops 1376010240 | bytes 12059136 | tf_op jit(solution)/shard_map/dot_general | solution.py:100
  205.5 5.5 %all-to-all-start.1 = ((bf16[32,4,1024]{2,1,0:T(4,128)(2,1)}), bf16[32,4,1024]{2,1,0:T(4,128)(2,1)S(1)}, u32[]{:S(2)}, u32[]{:S(2)}) async-start(bf16[32,4,1024]{2,1,0:T(4,128)(2,1)} %all_to_all.39), calls=%async_computation.1 | async-start | bytes 524288 | tf_op jit(solution)/shard_map/all_to_all | solution.py:105
  211.2 3.9 %copy.37 = bf16[1024,1024]{0,1:T(8,128)(2,1)} copy(bf16[1024,1024]{1,0:T(8,128)(2,1)} %param.13) | data formatting | bytes 4194304 | tf_op args[4]
  215.2 4.0 %copy.36 = bf16[1024,1024]{0,1:T(8,128)(2,1)} copy(bf16[1024,1024]{1,0:T(8,128)(2,1)} %param.12) | data formatting | bytes 4194304 | tf_op args[3]
  220.7 5.6 %multiply_reduce_fusion.1 = (f32[1024]{0:T(1024)S(1)}, f32[1024]{0:T(1024)S(1)}, f32[1024,1024]{0,1:T(8,128)}) fusion(bf16[1024,1024]{0,1:T(8,128)(2,1)} %copy.37, f32[1024]{0:T(1024)S(1)} %convert_element_type.80, bf16[1024,1024]{0,1:T(8,128)(2,1)} %copy.36, bf16[128,1024]{1,0:T(8,128)(2,1)S(1)} %all_to_all.41, s32[128]{0:T(128)S(1)} %eq.74, ...), kind=kOutput, calls=%fused_computation.5 | convolution fusion | flops 276953088 | bytes 8664576 | tf_op jit(solution)/shard_map/dot_general | solution.py:110
  226.3 13.8 %all_to_all.55 = f32[8,1,2048]{2,1,0:T(1,128)S(1)} all-to-all(f32[8,1,2048]{2,1,0:T(1,128)S(1)} %broadcast_in_dim.73), channel_id=1, replica_groups=mesh['ctx'=32,'tp'=8] {'tp'}, dimensions={0} | all-to-all | bytes 131072 | tf_op jit(solution)/shard_map/all_to_all | solution.py:16
  240.1 4.3 %fusion.6 = bf16[128,1024]{1,0:T(8,128)(2,1)S(1)} fusion(f32[1024,1024]{0,1:T(8,128)} %get-tuple-element.37, bf16[1024,1024]{0,1:T(8,128)(2,1)} %copy.37, f32[1024]{0:T(1024)S(1)} %get-tuple-element.34, f32[1024]{0:T(1024)S(1)} %get-tuple-element.32, f32[1024]{0:T(1024)S(1)} %get-tuple-element.33, f32[1024]{0:T(1024)S(1)} %convert_element_type.80, ...), kind=kOutput, calls=%fused_computation.17 | convolution fusion | flops 277217280 | bytes 6570496 | tf_op jit(solution)/shard_map/dot_general | solution.py:62
  244.5 17.6 %all_to_all.56 = bf16[32,4,1024]{2,1,0:T(4,128)(2,1)S(1)} all-to-all(bf16[32,4,1024]{2,1,0:T(4,128)(2,1)S(1)} %all_to_all.47), channel_id=1, replica_groups=mesh['ctx'=32,'tp'=8] {'ctx'}, dimensions={0} | all-to-all | bytes 524288 | tf_op jit(solution)/shard_map/all_to_all | solution.py:122
  263.2 3.6 %all_to_all.43 = bf16[128,32,160]{2,1,0:T(8,128)(2,1)} reshape(bf16[512,1280]{1,0:T(8,128)(2,1)S(1)} %add_convert_fusion) | data formatting | bytes 2621440 | tf_op jit(solution)/shard_map/all_to_all | solution.py:87
  266.8 4.4 %copy.39 = bf16[128,32,160]{0,2,1:T(8,128)(2,1)} copy(bf16[128,32,160]{2,1,0:T(8,128)(2,1)} %all_to_all.43) | data formatting | bytes 2621440 | tf_op jit(solution)/shard_map/all_to_all | solution.py:87
  271.2 4.5 %all-to-all-start.3 = ((bf16[128,32,160]{0,2,1:T(8,128)(2,1)}), bf16[128,32,160]{0,2,1:T(8,128)(2,1)}, u32[]{:S(2)}, u32[]{:S(2)}) async-start(bf16[128,32,160]{0,2,1:T(8,128)(2,1)} %copy.39), calls=%async_computation.3 | async-start | bytes 2621440 | tf_op jit(solution)/shard_map/all_to_all | solution.py:87
  275.7 2.6 multiply_convert_fusion
  278.3 2.6 copy.41
  280.9 15.4 %all-to-all-done.3 = bf16[128,32,160]{0,2,1:T(8,128)(2,1)} async-done(((bf16[128,32,160]{0,2,1:T(8,128)(2,1)}), bf16[128,32,160]{0,2,1:T(8,128)(2,1)}, u32[]{:S(2)}, u32[]{:S(2)}) %all-to-all-start.3) | async-done | bytes 1310752 | tf_op jit(solution)/shard_map/all_to_all | solution.py:87
  296.3 27.3 %all-gather.7.cloned.1.call-done = bf16[4096,1024]{1,0:T(8,128)(2,1)} async-done(((bf16[128,1024]{1,0:T(8,128)(2,1)}), bf16[4096,1024]{1,0:T(8,128)(2,1)}) %all-gather.7.cloned.1.call-update) | async-done | bytes 8388624 | tf_op jit(solution)/shard_map/all_gather | solution.py:125
  323.6 6.2 %fusion.3 = f32[160,1024]{1,0:T(8,128)} fusion(bf16[4096,1024]{1,0:T(8,128)(2,1)} %all-gather.7.cloned.1.call-done, bf16[128,32,160]{0,2,1:T(8,128)(2,1)} %all-to-all-done.3), kind=kOutput, calls=%fused_computation.14 | convolution fusion | flops 1342177280 | bytes 10354688 | tf_op jit(solution)/shard_map/dot_general | solution.py:62
  (47 shorter events, 11.0 us)
Async XLA Ops:
  7.2 8.3 %copy-start = (bf16[160,1280]{1,0:T(8,128)(2,1)S(1)}, bf16[160,1280]{1,0:T(8,128)(2,1)}, u32[]{:S(2)}) copy-start(bf16[160,1280]{1,0:T(8,128)(2,1)} %param.15) | copy-start | bytes 1228804
  7.2 4.1 %copy-start.1 = (bf16[512,1280]{1,0:T(8,128)(2,1)S(1)}, bf16[512,1280]{1,0:T(8,128)(2,1)}, u32[]{:S(2)}) copy-start(bf16[512,1280]{1,0:T(8,128)(2,1)} %param.9) | copy-start | bytes 3932164
  7.2 127.4 %all-gather.9.cloned.1.call-start = ((), (), s32[]{:S(2)}) async-start(), calls=%async_computation.7 | async-start | bytes 11796480 | tf_op jit(solution)/shard_map/all_gather | solution.py:11
  9.3 3.6 %copy-start.2 = (s32[512]{0:T(512)S(1)}, s32[512]{0:T(512)}, u32[]{:S(2)}) copy-start(s32[512]{0:T(512)} %param.10) | copy-start | bytes 6148
  15.4 2.4 copy-start.4
  17.1 182.0 %all-gather.5.cloned.1.call-start = ((), (), s32[]{:S(2)}) async-start(), calls=%async_computation.5 | async-start | bytes 10813440 | tf_op jit(solution)/shard_map/all_gather | solution.py:91
  19.3 186.2 %all-to-all-start = ((s32[32,4,1]{1,2,0:T(1,128)}), s32[32,4,1]{1,2,0:T(1,128)S(1)}, u32[]{:S(2)}, u32[]{:S(2)}) async-start(s32[32,4,1]{1,2,0:T(1,128)} %bitcast), calls=%async_computation | async-start | bytes 32768 | tf_op jit(solution)/shard_map/all_to_all | solution.py:106
  143.3 67.9 %copy-start.3 = (bf16[1024]{0:T(1024)(128)(2,1)S(1)}, bf16[1024]{0:T(1024)(128)(2,1)}, u32[]{:S(2)}) copy-start(bf16[1024]{0:T(1024)(128)(2,1)} %param.17) | copy-start | bytes 6148
  205.5 15.1 %all-to-all-start.1 = ((bf16[32,4,1024]{2,1,0:T(4,128)(2,1)}), bf16[32,4,1024]{2,1,0:T(4,128)(2,1)S(1)}, u32[]{:S(2)}, u32[]{:S(2)}) async-start(bf16[32,4,1024]{2,1,0:T(4,128)(2,1)} %all_to_all.39), calls=%async_computation.1 | async-start | bytes 524288 | tf_op jit(solution)/shard_map/all_to_all | solution.py:105
  211.0 112.6 %all-gather.7.cloned.1.call-start = ((), (), s32[]{:S(2)}) async-start(), calls=%async_computation.6 | async-start | bytes 8650752 | tf_op jit(solution)/shard_map/all_gather | solution.py:125
  271.2 25.1 %all-to-all-start.3 = ((bf16[128,32,160]{0,2,1:T(8,128)(2,1)}), bf16[128,32,160]{0,2,1:T(8,128)(2,1)}, u32[]{:S(2)}, u32[]{:S(2)}) async-start(bf16[128,32,160]{0,2,1:T(8,128)(2,1)} %copy.39), calls=%async_computation.3 | async-start | bytes 2621440 | tf_op jit(solution)/shard_map/all_to_all | solution.py:87
Sparse Core Ops, SparseCore 0:
  17.2 117.3 all-gather.8
  137.1 61.8 all-gather.4
  263.3 60.2 all-gather.6
